TPU v7x, 128 devices: a whole 4x4x4 slice. The times are simulated.
128 devices in a mesh: tasks: 1, group: 128 (over z, y, x, core).
Axes of the slice: x: 4, y: 4, z: 4, core: 2. Of those that a mesh axis runs over, the one named last changes fastest.
Arguments:
- points: bfloat16 [196608, 128], P(('tasks', 'group'))
- vectors: bfloat16 [196608, 64], P(('tasks', 'group'))
- lengthscale: float32 [1], replicated
- outscale: float32 [1], replicated
Outputs:
- output: float32 [196608, 64], P(('tasks', 'group'))
All inputs are finite; a program needn't handle non-finite values.
Results may differ from a plain program's by a relative error of at most 0.001.
Values are sent between devices in bfloat16 or wider.
A program may use at most 1 GiB of HBM per device.

v0:
```python
import jax
import jax.numpy as jnp
from jax import lax
from jax.sharding import PartitionSpec as P


def row_norms(x_rows):
    return jnp.sum(jnp.square(x_rows.astype(jnp.float32)), axis=1)


def kernel_block(x_rows, norm_rows, x_cols, norm_cols, two_ell_sq, out_scale):
    gram_mat = jnp.einsum('nd,md->nm', x_rows, x_cols, preferred_element_type=jnp.float32)
    sq_dist = jnp.maximum(norm_rows[:, None] + norm_cols[None, :] - 2.0 * gram_mat, 0.0)
    return (out_scale * jnp.exp(-sq_dist / two_ell_sq)).astype(jnp.bfloat16)


def solution(mesh):
    n_group = mesh.shape['group']
    half_way = n_group // 2
    shift_left = [(source_idx, (source_idx - 1) % n_group) for source_idx in range(n_group)]
    send_back = [(source_idx, (source_idx + half_way - 1) % n_group) for source_idx in range(n_group)]
    row_spec = P(('tasks', 'group'), None)

    def local_fn(x_loc, v_loc, lengthscale, outscale):
        two_ell_sq = 2.0 * jnp.square(lengthscale[0])
        out_scale = outscale[0]
        norm_loc = row_norms(x_loc)

        def pair_step(x_vis, v_vis, y_acc, partner_acc):
            kern_pair = kernel_block(x_loc, norm_loc, x_vis, row_norms(x_vis), two_ell_sq, out_scale)
            y_acc = y_acc + jnp.dot(kern_pair, v_vis, preferred_element_type=jnp.float32)
            partner_acc = partner_acc + jnp.einsum('nm,nr->mr', kern_pair, v_loc, preferred_element_type=jnp.float32)
            return y_acc, partner_acc

        def loop_body(step_idx, carry):
            x_vis, v_vis, y_acc, partner_acc = carry
            x_vis = lax.ppermute(x_vis, 'group', shift_left)
            v_vis = lax.ppermute(v_vis, 'group', shift_left)
            partner_acc = lax.ppermute(partner_acc, 'group', shift_left)
            y_acc, partner_acc = pair_step(x_vis, v_vis, y_acc, partner_acc)
            return x_vis, v_vis, y_acc, partner_acc

        kern_diag = kernel_block(x_loc, norm_loc, x_loc, norm_loc, two_ell_sq, out_scale)
        y_acc = jnp.dot(kern_diag, v_loc, preferred_element_type=jnp.float32)
        x_vis = lax.ppermute(x_loc, 'group', shift_left)
        v_vis = lax.ppermute(v_loc, 'group', shift_left)
        y_acc, partner_acc = pair_step(x_vis, v_vis, y_acc, jnp.zeros(y_acc.shape, jnp.float32))
        x_vis, v_vis, y_acc, partner_acc = lax.fori_loop(2, half_way, loop_body, (x_vis, v_vis, y_acc, partner_acc))
        y_acc = y_acc + lax.ppermute(partner_acc, 'group', send_back)
        x_vis = lax.ppermute(x_vis, 'group', shift_left)
        v_vis = lax.ppermute(v_vis, 'group', shift_left)
        kern_far = kernel_block(x_loc, norm_loc, x_vis, row_norms(x_vis), two_ell_sq, out_scale)
        return y_acc + jnp.dot(kern_far, v_vis, preferred_element_type=jnp.float32)

    return jax.shard_map(local_fn, mesh=mesh, in_specs=(row_spec, row_spec, P(None), P(None)), out_specs=row_spec, check_vma=False)
```

profile of v0, /device:TPU:0, one launch (start us, length us, event | category | flops | bytes accessed | tf_op | source)
XLA Modules:
  0.0 1561.9 jit_solution(884927507191215230)
XLA Ops:
  17.6 9.7 copy.6
  38.2 9.7 copy.8
  55.7 1471.2 %while.16 = (s32[]{:T(128)}, bf16[1536,128]{1,0:T(8,128)(2,1)S(1)}, bf16[1536,64]{1,0:T(8,128)(2,1)S(1)}, f32[1536,64]{0,1:T(8,128)S(1)}, f32[1536,64]{0,1:T(8,1...) while((s32[]{:T(128)}, bf16[1536,128]{1,0:T(8,128)(2,1)S(1)}, ...), condition=%wide.region_4.0_spmd, body=%wide.region_2.0_spmd.sunk | while | flops 1227618816 | bytes 22431980 | solution.py:48
  80.1 9.3 collective-permute-done.1
  103.9 9.3 collective-permute-done.1
  127.7 9.3 collective-permute-done.1
  151.5 9.3 collective-permute-done.1
  175.3 9.3 collective-permute-done.1
  199.1 9.3 collective-permute-done.1
  222.9 9.3 collective-permute-done.1
  246.7 9.3 collective-permute-done.1
  318.1 9.3 collective-permute-done.1
  413.3 9.3 collective-permute-done.1
  532.4 9.3 collective-permute-done.1
  651.4 9.3 collective-permute-done.1
  770.4 9.3 collective-permute-done.1
  865.7 9.3 collective-permute-done.1
  984.7 9.3 collective-permute-done.1
  1103.7 9.3 collective-permute-done.1
  1222.8 9.3 collective-permute-done.1
  1318.0 9.3 collective-permute-done.1
  1437.0 9.3 collective-permute-done.1
  1508.4 10.8 collective-permute-done.1
  1544.2 9.6 copy.9
  (750 shorter events, 1339.0 us)
Async XLA Ops:
  0.0 33.6 %collective-permute-start.3 = (bf16[1536,128]{1,0:T(8,128)(2,1)}, bf16[1536,128]{1,0:T(8,128)(2,1)S(1)}, u32[]{:S(2)}, u32[]{:S(2)}) collective-permute-start(bf16[1536,128]{1,0:T(8,128)(2,1)} %param.6), channel_id=1, source_target_pairs={{0,127},{1,0},{2,1},{3,2},{4,3},{5,4},{6,5},{7,6},{8,7},{9,8},{10,... | collective-permute-start | bytes 1179656 | tf_op jit(solution)/shard_map/ppermute | solution.py:45
  9.4 44.7 %collective-permute-start.4 = (bf16[1536,64]{1,0:T(8,128)(2,1)S(1)}, bf16[1536,64]{1,0:T(8,128)(2,1)S(1)}, u32[]{:S(2)}, u32[]{:S(2)}) collective-permute-start(bf16[1536,64]{1,0:T(8,128)(2,1)S(1)} %copy.5), channel_id=1, source_target_pairs={{0,127},{1,0},{2,1},{3,2},{4,3},{5,4},{6,5},{7,6},{8,7},{9,8},{10,... | collective-permute-start | bytes 589832 | tf_op jit(solution)/shard_map/ppermute | solution.py:46
  96.3 16.9 %collective-permute-start = (bf16[1536,128]{1,0:T(8,128)(2,1)S(1)}, bf16[1536,128]{1,0:T(8,128)(2,1)S(1)}, u32[]{:S(2)}, u32[]{:S(2)}) collective-permute-start(bf16[1536,128]{1,0:T(8,128)(2,1)S(1)} %get-tuple-element.157), channel_id=1, source_target_pairs={{0,127},{1,0},{2,1},{3,2},{4,3},{5,4},{6,5},{7,6},{8,7},{9,8},{10,... | collective-permute-start | bytes 1179656 | tf_op jit(solution)/shard_map/while/body/eval_jaxpr/ppermute | solution.py:37
  120.1 16.9 %collective-permute-start = (bf16[1536,128]{1,0:T(8,128)(2,1)S(1)}, bf16[1536,128]{1,0:T(8,128)(2,1)S(1)}, u32[]{:S(2)}, u32[]{:S(2)}) collective-permute-start(bf16[1536,128]{1,0:T(8,128)(2,1)S(1)} %get-tuple-element.157), channel_id=1, source_target_pairs={{0,127},{1,0},{2,1},{3,2},{4,3},{5,4},{6,5},{7,6},{8,7},{9,8},{10,... | collective-permute-start | bytes 1179656 | tf_op jit(solution)/shard_map/while/body/eval_jaxpr/ppermute | solution.py:37
  143.9 16.9 %collective-permute-start = (bf16[1536,128]{1,0:T(8,128)(2,1)S(1)}, bf16[1536,128]{1,0:T(8,128)(2,1)S(1)}, u32[]{:S(2)}, u32[]{:S(2)}) collective-permute-start(bf16[1536,128]{1,0:T(8,128)(2,1)S(1)} %get-tuple-element.157), channel_id=1, source_target_pairs={{0,127},{1,0},{2,1},{3,2},{4,3},{5,4},{6,5},{7,6},{8,7},{9,8},{10,... | collective-permute-start | bytes 1179656 | tf_op jit(solution)/shard_map/while/body/eval_jaxpr/ppermute | solution.py:37
  167.7 16.9 %collective-permute-start = (bf16[1536,128]{1,0:T(8,128)(2,1)S(1)}, bf16[1536,128]{1,0:T(8,128)(2,1)S(1)}, u32[]{:S(2)}, u32[]{:S(2)}) collective-permute-start(bf16[1536,128]{1,0:T(8,128)(2,1)S(1)} %get-tuple-element.157), channel_id=1, source_target_pairs={{0,127},{1,0},{2,1},{3,2},{4,3},{5,4},{6,5},{7,6},{8,7},{9,8},{10,... | collective-permute-start | bytes 1179656 | tf_op jit(solution)/shard_map/while/body/eval_jaxpr/ppermute | solution.py:37
  191.5 16.9 %collective-permute-start = (bf16[1536,128]{1,0:T(8,128)(2,1)S(1)}, bf16[1536,128]{1,0:T(8,128)(2,1)S(1)}, u32[]{:S(2)}, u32[]{:S(2)}) collective-permute-start(bf16[1536,128]{1,0:T(8,128)(2,1)S(1)} %get-tuple-element.157), channel_id=1, source_target_pairs={{0,127},{1,0},{2,1},{3,2},{4,3},{5,4},{6,5},{7,6},{8,7},{9,8},{10,... | collective-permute-start | bytes 1179656 | tf_op jit(solution)/shard_map/while/body/eval_jaxpr/ppermute | solution.py:37
  215.3 16.9 %collective-permute-start = (bf16[1536,128]{1,0:T(8,128)(2,1)S(1)}, bf16[1536,128]{1,0:T(8,128)(2,1)S(1)}, u32[]{:S(2)}, u32[]{:S(2)}) collective-permute-start(bf16[1536,128]{1,0:T(8,128)(2,1)S(1)} %get-tuple-element.157), channel_id=1, source_target_pairs={{0,127},{1,0},{2,1},{3,2},{4,3},{5,4},{6,5},{7,6},{8,7},{9,8},{10,... | collective-permute-start | bytes 1179656 | tf_op jit(solution)/shard_map/while/body/eval_jaxpr/ppermute | solution.py:37
  239.1 16.9 %collective-permute-start = (bf16[1536,128]{1,0:T(8,128)(2,1)S(1)}, bf16[1536,128]{1,0:T(8,128)(2,1)S(1)}, u32[]{:S(2)}, u32[]{:S(2)}) collective-permute-start(bf16[1536,128]{1,0:T(8,128)(2,1)S(1)} %get-tuple-element.157), channel_id=1, source_target_pairs={{0,127},{1,0},{2,1},{3,2},{4,3},{5,4},{6,5},{7,6},{8,7},{9,8},{10,... | collective-permute-start | bytes 1179656 | tf_op jit(solution)/shard_map/while/body/eval_jaxpr/ppermute | solution.py:37
  262.9 16.9 %collective-permute-start = (bf16[1536,128]{1,0:T(8,128)(2,1)S(1)}, bf16[1536,128]{1,0:T(8,128)(2,1)S(1)}, u32[]{:S(2)}, u32[]{:S(2)}) collective-permute-start(bf16[1536,128]{1,0:T(8,128)(2,1)S(1)} %get-tuple-element.157), channel_id=1, source_target_pairs={{0,127},{1,0},{2,1},{3,2},{4,3},{5,4},{6,5},{7,6},{8,7},{9,8},{10,... | collective-permute-start | bytes 1179656 | tf_op jit(solution)/shard_map/while/body/eval_jaxpr/ppermute | solution.py:37
  286.7 16.9 %collective-permute-start = (bf16[1536,128]{1,0:T(8,128)(2,1)S(1)}, bf16[1536,128]{1,0:T(8,128)(2,1)S(1)}, u32[]{:S(2)}, u32[]{:S(2)}) collective-permute-start(bf16[1536,128]{1,0:T(8,128)(2,1)S(1)} %get-tuple-element.157), channel_id=1, source_target_pairs={{0,127},{1,0},{2,1},{3,2},{4,3},{5,4},{6,5},{7,6},{8,7},{9,8},{10,... | collective-permute-start | bytes 1179656 | tf_op jit(solution)/shard_map/while/body/eval_jaxpr/ppermute | solution.py:37
  310.5 16.9 %collective-permute-start = (bf16[1536,128]{1,0:T(8,128)(2,1)S(1)}, bf16[1536,128]{1,0:T(8,128)(2,1)S(1)}, u32[]{:S(2)}, u32[]{:S(2)}) collective-permute-start(bf16[1536,128]{1,0:T(8,128)(2,1)S(1)} %get-tuple-element.157), channel_id=1, source_target_pairs={{0,127},{1,0},{2,1},{3,2},{4,3},{5,4},{6,5},{7,6},{8,7},{9,8},{10,... | collective-permute-start | bytes 1179656 | tf_op jit(solution)/shard_map/while/body/eval_jaxpr/ppermute | solution.py:37
  334.3 16.9 %collective-permute-start = (bf16[1536,128]{1,0:T(8,128)(2,1)S(1)}, bf16[1536,128]{1,0:T(8,128)(2,1)S(1)}, u32[]{:S(2)}, u32[]{:S(2)}) collective-permute-start(bf16[1536,128]{1,0:T(8,128)(2,1)S(1)} %get-tuple-element.157), channel_id=1, source_target_pairs={{0,127},{1,0},{2,1},{3,2},{4,3},{5,4},{6,5},{7,6},{8,7},{9,8},{10,... | collective-permute-start | bytes 1179656 | tf_op jit(solution)/shard_map/while/body/eval_jaxpr/ppermute | solution.py:37
  358.1 16.9 %collective-permute-start = (bf16[1536,128]{1,0:T(8,128)(2,1)S(1)}, bf16[1536,128]{1,0:T(8,128)(2,1)S(1)}, u32[]{:S(2)}, u32[]{:S(2)}) collective-permute-start(bf16[1536,128]{1,0:T(8,128)(2,1)S(1)} %get-tuple-element.157), channel_id=1, source_target_pairs={{0,127},{1,0},{2,1},{3,2},{4,3},{5,4},{6,5},{7,6},{8,7},{9,8},{10,... | collective-permute-start | bytes 1179656 | tf_op jit(solution)/shard_map/while/body/eval_jaxpr/ppermute | solution.py:37
  381.9 16.9 %collective-permute-start = (bf16[1536,128]{1,0:T(8,128)(2,1)S(1)}, bf16[1536,128]{1,0:T(8,128)(2,1)S(1)}, u32[]{:S(2)}, u32[]{:S(2)}) collective-permute-start(bf16[1536,128]{1,0:T(8,128)(2,1)S(1)} %get-tuple-element.157), channel_id=1, source_target_pairs={{0,127},{1,0},{2,1},{3,2},{4,3},{5,4},{6,5},{7,6},{8,7},{9,8},{10,... | collective-permute-start | bytes 1179656 | tf_op jit(solution)/shard_map/while/body/eval_jaxpr/ppermute | solution.py:37
  405.7 16.9 %collective-permute-start = (bf16[1536,128]{1,0:T(8,128)(2,1)S(1)}, bf16[1536,128]{1,0:T(8,128)(2,1)S(1)}, u32[]{:S(2)}, u32[]{:S(2)}) collective-permute-start(bf16[1536,128]{1,0:T(8,128)(2,1)S(1)} %get-tuple-element.157), channel_id=1, source_target_pairs={{0,127},{1,0},{2,1},{3,2},{4,3},{5,4},{6,5},{7,6},{8,7},{9,8},{10,... | collective-permute-start | bytes 1179656 | tf_op jit(solution)/shard_map/while/body/eval_jaxpr/ppermute | solution.py:37
  429.6 16.9 %collective-permute-start = (bf16[1536,128]{1,0:T(8,128)(2,1)S(1)}, bf16[1536,128]{1,0:T(8,128)(2,1)S(1)}, u32[]{:S(2)}, u32[]{:S(2)}) collective-permute-start(bf16[1536,128]{1,0:T(8,128)(2,1)S(1)} %get-tuple-element.157), channel_id=1, source_target_pairs={{0,127},{1,0},{2,1},{3,2},{4,3},{5,4},{6,5},{7,6},{8,7},{9,8},{10,... | collective-permute-start | bytes 1179656 | tf_op jit(solution)/shard_map/while/body/eval_jaxpr/ppermute | solution.py:37
  453.4 16.9 %collective-permute-start = (bf16[1536,128]{1,0:T(8,128)(2,1)S(1)}, bf16[1536,128]{1,0:T(8,128)(2,1)S(1)}, u32[]{:S(2)}, u32[]{:S(2)}) collective-permute-start(bf16[1536,128]{1,0:T(8,128)(2,1)S(1)} %get-tuple-element.157), channel_id=1, source_target_pairs={{0,127},{1,0},{2,1},{3,2},{4,3},{5,4},{6,5},{7,6},{8,7},{9,8},{10,... | collective-permute-start | bytes 1179656 | tf_op jit(solution)/shard_map/while/body/eval_jaxpr/ppermute | solution.py:37
  477.2 16.9 %collective-permute-start = (bf16[1536,128]{1,0:T(8,128)(2,1)S(1)}, bf16[1536,128]{1,0:T(8,128)(2,1)S(1)}, u32[]{:S(2)}, u32[]{:S(2)}) collective-permute-start(bf16[1536,128]{1,0:T(8,128)(2,1)S(1)} %get-tuple-element.157), channel_id=1, source_target_pairs={{0,127},{1,0},{2,1},{3,2},{4,3},{5,4},{6,5},{7,6},{8,7},{9,8},{10,... | collective-permute-start | bytes 1179656 | tf_op jit(solution)/shard_map/while/body/eval_jaxpr/ppermute | solution.py:37
  501.0 16.9 %collective-permute-start = (bf16[1536,128]{1,0:T(8,128)(2,1)S(1)}, bf16[1536,128]{1,0:T(8,128)(2,1)S(1)}, u32[]{:S(2)}, u32[]{:S(2)}) collective-permute-start(bf16[1536,128]{1,0:T(8,128)(2,1)S(1)} %get-tuple-element.157), channel_id=1, source_target_pairs={{0,127},{1,0},{2,1},{3,2},{4,3},{5,4},{6,5},{7,6},{8,7},{9,8},{10,... | collective-permute-start | bytes 1179656 | tf_op jit(solution)/shard_map/while/body/eval_jaxpr/ppermute | solution.py:37
  1500.8 18.4 %collective-permute-start = (bf16[1536,128]{1,0:T(8,128)(2,1)S(1)}, bf16[1536,128]{1,0:T(8,128)(2,1)S(1)}, u32[]{:S(2)}, u32[]{:S(2)}) collective-permute-start(bf16[1536,128]{1,0:T(8,128)(2,1)S(1)} %get-tuple-element.157), channel_id=1, source_target_pairs={{0,127},{1,0},{2,1},{3,2},{4,3},{5,4},{6,5},{7,6},{8,7},{9,8},{10,... | collective-permute-start | bytes 1179656 | tf_op jit(solution)/shard_map/while/body/eval_jaxpr/ppermute | solution.py:37
  1508.3 17.6 %collective-permute-start.2 = (f32[1536,64]{0,1:T(8,128)S(1)}, f32[1536,64]{0,1:T(8,128)S(1)}, u32[]{:S(2)}, u32[]{:S(2)}) collective-permute-start(f32[1536,64]{0,1:T(8,128)S(1)} %get-tuple-element.160), channel_id=1, source_target_pairs={{0,127},{1,0},{2,1},{3,2},{4,3},{5,4},{6,5},{7,6},{8,7},{9,8},{10,... | collective-permute-start | bytes 1179656 | tf_op jit(solution)/shard_map/while/body/eval_jaxpr/ppermute | solution.py:39
  1534.3 19.5 %collective-permute-start.5 = (f32[1536,64]{0,1:T(8,128)S(1)}, f32[1536,64]{0,1:T(8,128)S(1)}, u32[]{:S(2)}, u32[]{:S(2)}) collective-permute-start(f32[1536,64]{0,1:T(8,128)S(1)} %get-tuple-element.61), channel_id=1, source_target_pairs={{0,63},{1,64},{2,65},{3,66},{4,67},{5,68},{6,69},{7,70},{8,71},{9,... | collective-permute-start | bytes 1179656 | tf_op jit(solution)/shard_map/ppermute | solution.py:49
  1534.3 19.5 %collective-permute-start.7 = (bf16[1536,64]{1,0:T(8,128)(2,1)S(1)}, bf16[1536,64]{1,0:T(8,128)(2,1)S(1)}, u32[]{:S(2)}, u32[]{:S(2)}) collective-permute-start(bf16[1536,64]{1,0:T(8,128)(2,1)S(1)} %get-tuple-element.63), channel_id=1, source_target_pairs={{0,127},{1,0},{2,1},{3,2},{4,3},{5,4},{6,5},{7,6},{8,7},{9,8},{10,... | collective-permute-start | bytes 589832 | tf_op jit(solution)/shard_map/ppermute | solution.py:51
  (169 other events, 2279.8 us)
where the time goes:
time: 1560 us
  waiting for transfers between devices  585 us (38%)
  starting transfers between devices  481 us (31%)
  matrix products  429 us (28%)
  local copies, waits for them, and re-layouts  33.4 us (2%)
  other arithmetic  27.6 us (2%)
    ppermute x62, waiting for transfers between devices, loop_body(): v_vis = lax.ppermute(v_vis, 'group', shift_left)  579 us
    ppermute x62, starting transfers between devices, loop_body(): x_vis = lax.ppermute(x_vis, 'group', shift_left)  453 us
    dot_general x64, matrix products, kernel_block(): jnp.einsum('nd,md->nm', x_rows, x_cols, preferred_element_type=jnp.float32)  259 us
    dot_general x63, matrix products, pair_step(): jnp.dot(kern_pair, v_vis, preferred_element_type=jnp.float32)  98.1 us
    dot_general x63, matrix products, pair_step(): jnp.einsum('nm,nr->mr', kern_pair, v_loc, preferred_element_type=jnp.floa...  58.4 us
  transfers between devices with their start and end apart: 191, of which 64 were waited for; matrix products, arithmetic and copies ran while one was open for 27% of the time, Pallas kernels for 0%

commit v1 on v0

v1 whole, which is shorter than its diff:
```python
import functools

import jax
import jax.numpy as jnp
from jax import lax
from jax.experimental import pallas as pl
from jax.experimental.pallas import tpu as pltpu
from jax.sharding import PartitionSpec as P

OFFSETS = (0, 6, 7, 21, 26, 31, 33, 37, 49, 53, 73, 88, 96, 97)
ROWS = 1536
HALF = 768
TILE = 256
FEAT = 128
RHS = 64
F32 = jnp.float32
BF16 = jnp.bfloat16


def coords(g):
    return (g // 32, (g // 8) % 4, (g // 2) % 4, g % 2)


def difference(a, b):
    ca, cb = coords(a), coords(b)
    z, y, x = ((ca[k] - cb[k]) % 4 for k in range(3))
    return ((z * 4 + y) * 4 + x) * 2 + (ca[3] - cb[3]) % 2


def hops(g):
    return sum(min(v, 4 - v) for v in coords(g)[:3])


def make_plan():
    offsets = sorted(OFFSETS, key=lambda a: (hops(a), a))
    n_slots = len(offsets)
    units = [(0, 0, 6, 1), (0, 0, 7, 0)]
    seen = {0}
    for n in range(1, n_slots):
        first = True
        for m in range(n):
            g, back = difference(offsets[n], offsets[m]), difference(offsets[m], offsets[n])
            if g in seen:
                continue
            seen.update((g, back))
            if g == back:
                kinds = (2 + [k for k in range(4) if coords(g)[k]][0],)
            else:
                kinds = (0, 1)
            for kind in kinds:
                units.append((n, m, kind, 1 if first else 0))
                first = False
        assert not first
    assert len(seen) == 128
    last = {}
    for idx, (i, j, _, _) in enumerate(units):
        last[i] = idx
        last[j] = idx
    done = {}
    for slot, idx in last.items():
        if slot:
            done.setdefault(idx, []).append(slot)
    codes = []
    for idx, (i, j, kind, new) in enumerate(units):
        ready = done.get(idx, [])
        assert set(ready) <= {i, j}
        codes.append(i + 16 * j + 256 * kind + 2048 * new + 4096 * (i in ready) + 8192 * (j in ready and i != j))
    return offsets, codes


def pick(values, idx):
    out = jnp.int32(values[0])
    for k in range(1, len(values)):
        out = jnp.where(idx == k, jnp.int32(values[k]), out)
    return out


def kernel(offsets, codes, c_ref, s_ref, x_ref, v_ref, out_ref, xs, vts, xl, xt, yt, yrecv, kb, kt,
           xsend, vsend, xrecv, vrecv, ysend, ysem):
    n_slots = len(offsets)
    me = lax.axis_index('group')
    core, px, py, pz = me % 2, (me // 2) % 4, (me // 8) % 4, me // 32
    scale = c_ref[0]
    out_scale = s_ref[0]

    def shifted(z, y, x, c):
        return ((((pz + z) % 4) * 4 + (py + y) % 4) * 4 + (px + x) % 4) * 2 + (core + c) % 2

    def plus(a):
        return shifted(*coords(a))

    def minus(a):
        z, y, x, c = coords(a)
        return shifted((4 - z) % 4, (4 - y) % 4, (4 - x) % 4, c)

    partners = sorted(set(offsets[1:]) | {difference(0, a) for a in offsets[1:]})
    barrier = pltpu.get_barrier_semaphore()
    for a in partners:
        pl.semaphore_signal(barrier, inc=1, device_id=(0, plus(a)), device_id_type=pl.DeviceIdType.MESH)
    pl.semaphore_wait(barrier, len(partners))

    def x_copy(slot, target):
        return pltpu.make_async_remote_copy(
            src_ref=x_ref, dst_ref=xs.at[slot], send_sem=xsend.at[slot], recv_sem=xrecv.at[slot],
            device_id=(0, target), device_id_type=pl.DeviceIdType.MESH)

    def v_copy(slot, target):
        return pltpu.make_async_remote_copy(
            src_ref=v_ref, dst_ref=vts.at[slot], send_sem=vsend.at[slot], recv_sem=vrecv.at[slot],
            device_id=(0, target), device_id_type=pl.DeviceIdType.MESH)

    def y_copy(slot, target):
        return pltpu.make_async_remote_copy(
            src_ref=yt.at[slot], dst_ref=yrecv.at[slot], send_sem=ysend.at[slot], recv_sem=ysem.at[slot],
            device_id=(0, target), device_id_type=pl.DeviceIdType.MESH)

    for slot in range(1, n_slots):
        x_copy(slot, minus(offsets[slot])).start()
        v_copy(slot, minus(offsets[slot])).start()

    xs[0] = x_ref[...]
    vts[0] = v_ref[...]
    for slot in range(n_slots + 1):
        yt[slot] = jnp.zeros((RHS, ROWS), F32)

    lane = lax.broadcasted_iota(jnp.int32, (TILE, FEAT), 1)

    def prepare(slot):
        for t in range(ROWS // TILE):
            rows = slice(t * TILE, (t + 1) * TILE)
            x = xs[slot, rows, :]
            xf = x.astype(F32)
            norm = jnp.broadcast_to(jnp.sum(xf * xf, axis=1, keepdims=True), (TILE, FEAT))
            hi = norm.astype(BF16).astype(F32)
            mid = (norm - hi).astype(BF16).astype(F32)
            low = norm - hi - mid
            parts_at = lambda k: jnp.where(lane == k, hi, jnp.where(lane == k + 1, mid, low))
            left = jnp.where(lane < 3, 1.0, jnp.where(lane < 6, parts_at(3), 0.0)).astype(BF16)
            right = jnp.where(lane < 3, parts_at(0), jnp.where(lane < 6, 1.0, 0.0)).astype(BF16)
            xl[slot, rows, 0:FEAT] = x * BF16(-2.0)
            xl[slot, rows, FEAT:2 * FEAT] = left
            xt[slot, 0:FEAT, rows] = x.T
            xt[slot, FEAT:2 * FEAT, rows] = right.T

    def unit(i, j, h, y_i):
        start = pl.multiple_of(h * HALF, HALF)
        for jc in range(ROWS // TILE):
            cols = slice(jc * TILE, (jc + 1) * TILE)
            right = xt[j, :, cols]
            for ic in range(HALF // TILE):
                rows = slice(ic * TILE, (ic + 1) * TILE)
                left = xl[i, pl.ds(pl.multiple_of(start + ic * TILE, TILE), TILE), :]
                dist = jnp.maximum(jnp.dot(left, right, preferred_element_type=F32), 0.0)
                kern = (jnp.exp2(dist * scale) * out_scale).astype(BF16)
                kb[rows, cols] = kern
                kt[cols, rows] = kern.T
        v_i = vts[i, :, pl.ds(start, HALF)]
        for jc in range(ROWS // TILE):
            cols = slice(jc * TILE, (jc + 1) * TILE)
            yt[j, :, cols] += jnp.dot(v_i, kb[:, cols], preferred_element_type=F32)
        yt[y_i, :, pl.ds(start, HALF)] += jnp.dot(vts[j], kt[...], preferred_element_type=F32)

    def send_partial(slot):
        target = shifted(*(pick([coords(a)[k] for a in offsets], slot) for k in range(4)))
        y_copy(slot, target).start()

    per_word = 2
    words = [sum(code << (14 * r) for r, code in enumerate(codes[w:w + per_word]))
             for w in range(0, len(codes), per_word)]
    per_block = 6
    n_blocks = -(-len(words) // per_block)
    words += [0] * (n_blocks * per_block - len(words))

    def block(b, _):
        picked = [pick(words[r::per_block], b) for r in range(per_block)]
        count = jnp.minimum(len(codes) - b * (per_block * per_word), per_block * per_word)

        def step(q, ws):
            code = ws[0] % 16384
            odd = q % 2 == 1
            ws = tuple(jnp.where(odd, ws[r + 1] if r + 1 < per_block else 0, ws[r] if r else ws[0] // 16384)
                       for r in range(per_block))
            n, m, kind = code % 16, (code // 16) % 16, (code // 256) % 8
            new, done_i, done_j = (code // 2048) % 2, (code // 4096) % 2, (code // 8192) % 2
            bit = jnp.where(kind == 2, pz // 2, jnp.where(kind == 3, py // 2, jnp.where(kind == 4, px // 2, core)))
            shared = (kind >= 2) & (kind < 6)
            swap = shared & (bit == 1)
            i = jnp.where(swap, m, n)
            j = jnp.where(swap, n, m)
            h = jnp.where(shared, bit, kind % 2)
            y_i = jnp.where(kind >= 6, n_slots, i)

            @pl.when(new == 1)
            def _():
                @pl.when(n > 0)
                def _():
                    x_copy(n, me).wait_recv()
                    v_copy(n, me).wait_recv()
                prepare(n)

            unit(i, j, h, y_i)

            @pl.when(done_i == 1)
            def _():
                send_partial(n)

            @pl.when(done_j == 1)
            def _():
                send_partial(m)

            return ws

        lax.fori_loop(0, count, step, tuple(picked))
        return 0

    lax.fori_loop(0, n_blocks, block, 0)

    out_ref[...] = yt[0]
    for slot in range(1, n_slots):
        y_copy(slot, me).wait_recv()
        out_ref[...] += yrecv[slot]
    for slot in range(1, n_slots):
        x_copy(slot, me).wait_send()
        v_copy(slot, me).wait_send()
        y_copy(slot, me).wait_send()


def solution(mesh):
    row_spec = P(('tasks', 'group'), None)
    offsets, codes = make_plan()
    n_slots = len(offsets)

    def local_fn(x_loc, v_loc, lengthscale, outscale):
        scale = -1.4426950408889634 / (2.0 * jnp.square(lengthscale))
        smem = pl.BlockSpec(memory_space=pltpu.SMEM)
        vmem = pl.BlockSpec(memory_space=pltpu.VMEM)
        dma = pltpu.SemaphoreType.DMA((n_slots,))
        y_t = pl.pallas_call(
            functools.partial(kernel, offsets, codes),
            out_shape=jax.ShapeDtypeStruct((RHS, ROWS), F32),
            in_specs=[smem, smem, vmem, vmem],
            out_specs=vmem,
            scratch_shapes=[
                pltpu.VMEM((n_slots, ROWS, FEAT), BF16),
                pltpu.VMEM((n_slots, RHS, ROWS), BF16),
                pltpu.VMEM((n_slots, ROWS, 2 * FEAT), BF16),
                pltpu.VMEM((n_slots, 2 * FEAT, ROWS), BF16),
                pltpu.VMEM((n_slots + 1, RHS, ROWS), F32),
                pltpu.VMEM((n_slots, RHS, ROWS), F32),
                pltpu.VMEM((HALF, ROWS), BF16),
                pltpu.VMEM((ROWS, HALF), BF16),
                dma, dma, dma, dma, dma, dma,
            ],
            compiler_params=pltpu.CompilerParams(
                collective_id=0, has_side_effects=True, vmem_limit_bytes=60 * 1024 * 1024),
        )(scale, outscale, x_loc, v_loc.T)
        return y_t.T

    return jax.shard_map(local_fn, mesh=mesh, in_specs=(row_spec, row_spec, P(None), P(None)),
                         out_specs=row_spec, check_vma=False)
```

time: 1560 us -> 320 us (0.21)
  the two profiles are of different devices: /device:TPU:0 before, /device:TPU:31 now
where the time goes in v1:
time: 320 us
  Pallas kernels  317 us (99%)
    pallas_call x1, Pallas kernels, local_fn(): pl.pallas_call(functools.partial(kernel, offsets, codes), out_shape=jax.S...  317 us

profile of v1, /device:TPU:31, one launch (start us, length us, event | category | flops | bytes accessed | tf_op | source)
XLA Modules:
  0.0 320.3 jit_solution(13077092541411171658)
XLA Ops:
  1.3 317.2 %shard_map.46 = f32[64,1536]{1,0:T(8,128)} custom-call(f32[1]{0:T(128)S(6)} %div.3.c_ref, f32[1]{0:T(128)S(6)} %copy.7.s_ref, bf16[1536,128]{1,0:T(8,128)(2,1)} %x_ref.1, bf16[64,1536]{1,0:T(8,128)(2,1)} %bitcast.3), custom_call_target="tpu_custom_call" | custom-call | tf_op jit(solution)/shard_map/pallas_call | solution.py:238
  318.5 1.8 copy.8

commit v2 on v1

v2 whole, which is shorter than its diff:
```python
import functools

import jax
import jax.numpy as jnp
from jax import lax
from jax.experimental import pallas as pl
from jax.experimental.pallas import tpu as pltpu
from jax.sharding import PartitionSpec as P

OFFSETS = (0, 6, 7, 21, 26, 31, 33, 37, 49, 53, 73, 88, 96, 97)
ROWS = 1536
HALF = 768
UNROLL = 3
LAG = 8
STEPS = 18
PANEL = 128
TILE = 256
FEAT = 128
RHS = 64
F32 = jnp.float32
BF16 = jnp.bfloat16


def coords(g):
    return (g // 32, (g // 8) % 4, (g // 2) % 4, g % 2)


def difference(a, b):
    ca, cb = coords(a), coords(b)
    z, y, x = ((ca[k] - cb[k]) % 4 for k in range(3))
    return ((z * 4 + y) * 4 + x) * 2 + (ca[3] - cb[3]) % 2


def hops(g):
    return sum(min(v, 4 - v) for v in coords(g)[:3])


def make_plan():
    offsets = sorted(OFFSETS, key=lambda a: (hops(a), a))
    n_slots = len(offsets)
    units = [(0, 0, 6, 1), (0, 0, 7, 0)]
    seen = {0}
    for n in range(1, n_slots):
        first = True
        for m in range(n):
            g, back = difference(offsets[n], offsets[m]), difference(offsets[m], offsets[n])
            if g in seen:
                continue
            seen.update((g, back))
            if g == back:
                kinds = (2 + [k for k in range(4) if coords(g)[k]][0],)
            else:
                kinds = (0, 1)
            for kind in kinds:
                units.append((n, m, kind, 1 if first else 0))
                first = False
        assert not first
    assert len(seen) == 128
    while len(units) % UNROLL:
        units.append((0, 0, 6, 0))
    trips = [units[t:t + UNROLL] for t in range(0, len(units), UNROLL)]
    last = {}
    for t, trip in enumerate(trips):
        for i, j, _, _ in trip:
            last[i] = t
            last[j] = t
    finished = sorted(range(1, n_slots), key=lambda slot: (last[slot], slot))
    words = []
    need = 1
    for t, trip in enumerate(trips):
        need = max([need] + [max(i, j) + 1 for i, j, _, _ in trip])
        sent = sum(last[slot] < t for slot in finished)
        codes = [i + 16 * j + 256 * kind for i, j, kind, _ in trip]
        words.append((codes[0] + 2048 * codes[1] + 2 ** 22 * need, codes[2] + 2048 * sent))
    return offsets, finished, words


def pick(values, idx):
    out = jnp.int32(values[0])
    for k in range(1, len(values)):
        out = jnp.where(idx == k, jnp.int32(values[k]), out)
    return out


def wide(a, b):
    return jnp.concatenate([a, b], axis=1)


def kernel(offsets, finished, words, c_ref, s_ref, x_ref, v_ref, out_ref, xs, vts, xl, xt, yt, yrecv, kb, kt,
           xsend, vsend, xrecv, vrecv, ysend, ysem):
    n_slots = len(offsets)
    me = lax.axis_index('group')
    core, px, py, pz = me % 2, (me // 2) % 4, (me // 8) % 4, me // 32
    scale = c_ref[0]
    out_scale = s_ref[0]

    def shifted(z, y, x, c):
        return ((((pz + z) % 4) * 4 + (py + y) % 4) * 4 + (px + x) % 4) * 2 + (core + c) % 2

    def plus(a):
        return shifted(*coords(a))

    def minus(a):
        z, y, x, c = coords(a)
        return shifted((4 - z) % 4, (4 - y) % 4, (4 - x) % 4, c)

    partners = sorted(set(offsets[1:]) | {difference(0, a) for a in offsets[1:]})
    barrier = pltpu.get_barrier_semaphore()
    for a in partners:
        pl.semaphore_signal(barrier, inc=1, device_id=(0, plus(a)), device_id_type=pl.DeviceIdType.MESH)
    pl.semaphore_wait(barrier, len(partners))

    def x_copy(slot, target):
        return pltpu.make_async_remote_copy(
            src_ref=x_ref, dst_ref=xs.at[slot], send_sem=xsend.at[slot], recv_sem=xrecv.at[slot],
            device_id=(0, target), device_id_type=pl.DeviceIdType.MESH)

    def v_copy(slot, target):
        return pltpu.make_async_remote_copy(
            src_ref=v_ref, dst_ref=vts.at[slot], send_sem=vsend.at[slot], recv_sem=vrecv.at[slot],
            device_id=(0, target), device_id_type=pl.DeviceIdType.MESH)

    def y_copy(slot, target):
        return pltpu.make_async_remote_copy(
            src_ref=yt.at[slot], dst_ref=yrecv.at[slot], send_sem=ysend.at[slot], recv_sem=ysem.at[slot],
            device_id=(0, target), device_id_type=pl.DeviceIdType.MESH)

    for slot in range(1, n_slots):
        x_copy(slot, minus(offsets[slot])).start()
        v_copy(slot, minus(offsets[slot])).start()

    xs[0] = x_ref[...]
    vts[0] = v_ref[...]
    kb[...] = jnp.zeros_like(kb)
    kt[...] = jnp.zeros_like(kt)

    def clear(slot, _):
        yt[slot] = jnp.zeros((RHS, ROWS), F32)
        for t in range(ROWS // PANEL):
            xt[lax.min(slot, n_slots - 1), t, FEAT + 16:2 * FEAT, :] = jnp.zeros((FEAT - 16, PANEL), BF16)
        return 0

    lax.fori_loop(0, n_slots + 1, clear, 0)
    row = lax.broadcasted_iota(jnp.int32, (16, PANEL), 0)
    nothing = jnp.zeros((FEAT - 16, PANEL), F32)

    def prepare(slot):
        for t in range(ROWS // PANEL):
            rows = slice(t * PANEL, (t + 1) * PANEL)
            x = xs[slot, rows, :]
            turned = x.T
            xf = turned.astype(F32)
            norm = jnp.sum(xf * xf, axis=0, keepdims=True)
            hi = norm.astype(BF16).astype(F32)
            mid = (norm - hi).astype(BF16).astype(F32)
            low = norm - hi - mid
            three = lambda k: jnp.where(row == k, hi, jnp.where(row == k + 1, mid, low))
            right = jnp.where(row < 3, three(0), jnp.where(row < 6, 1.0, 0.0))
            left = jnp.where(row < 3, 1.0, jnp.where(row < 6, three(3), 0.0))
            xt[slot, t, 0:FEAT, :] = turned
            xt[slot, t, FEAT:FEAT + 16, :] = right.astype(BF16)
            xl[slot, 0, rows, :] = x * BF16(-2.0)
            xl[slot, 1, rows, :] = jnp.concatenate([left, nothing], axis=0).astype(BF16).T

    def arrive(slot, _):
        x_copy(slot, me).wait_recv()
        v_copy(slot, me).wait_recv()
        prepare(slot)
        return 0

    def send_partial(k, _):
        slot = pick(finished, k)
        target = shifted(*(pick([coords(a)[axis] for a in offsets], slot) for axis in range(4)))
        y_copy(slot, target).start()
        return 0

    def decode(code):
        n, m, kind = code % 16, (code // 16) % 16, (code // 256) % 8
        bit = jnp.where(kind == 2, pz // 2, jnp.where(kind == 3, py // 2, jnp.where(kind == 4, px // 2, core)))
        shared = (kind >= 2) & (kind < 6)
        swap = shared & (bit == 1)
        i = jnp.where(swap, m, n)
        j = jnp.where(swap, n, m)
        return i, j, jnp.where(shared, bit, kind % 2), jnp.where(kind >= 6, n_slots, i), j

    parts_i, parts_j = {}, {}

    def add(parts, key, value):
        parts[key] = parts[key] + value if key in parts else value

    def place(step):
        pair, q = divmod(step, 2)
        return 2 * (pair // 3) + q, pair % 3

    def products(step, who):
        i, j, h = who[:3]
        jc, ic = place(step)
        panel = h * 6 + 2 * ic
        add(parts_j, jc, jnp.dot(wide(vts[i, panel], vts[i, panel + 1]), wide(kb[step, 0], kb[step, 1]),
                                 preferred_element_type=F32))
        add(parts_i, ic, jnp.dot(wide(vts[j, 2 * jc], vts[j, 2 * jc + 1]), wide(kt[step, 0], kt[step, 1]),
                                 preferred_element_type=F32))

    def finish_cols(jc, who):
        if jc in parts_j:
            yt[who[4], :, jc * TILE:(jc + 1) * TILE] += parts_j.pop(jc)

    def finish_rows(who):
        for ic in sorted(parts_i):
            cols = pl.ds(pl.multiple_of(who[2] * HALF + ic * TILE, TILE), TILE)
            yt[who[3], :, cols] += parts_i.pop(ic)

    def finish_all(who):
        for jc in sorted(parts_j):
            finish_cols(jc, who)
        finish_rows(who)

    def unit(who, before):
        i, j, h = who[:3]
        for step in range(STEPS):
            jc, ic = place(step)
            rows = pl.ds(pl.multiple_of(h * HALF + ic * TILE, TILE), TILE)
            dist = jnp.dot(wide(xl[i, 0, rows, :], xl[i, 1, rows, :]), wide(xt[j, 2 * jc], xt[j, 2 * jc + 1]),
                           preferred_element_type=F32)
            late = (step - LAG) % STEPS
            owner = who if step >= LAG else before
            products(late, owner)
            if place(late)[1] == 2:
                finish_cols(place(late)[0], owner)
            if step == LAG - 1:
                finish_rows(before)
            kern = (jnp.exp2(jnp.maximum(dist, 0.0) * scale) * out_scale).astype(BF16)
            turned = kern.T
            for e in range(2):
                cols = slice(e * PANEL, (e + 1) * PANEL)
                kb[step, e] = kern[:, cols]
                kt[step, e] = turned[:, cols]

    def trip(t, carry):
        have, sent, before = carry[0], carry[1], carry[2:]
        first, second = pick([w[0] for w in words], t), pick([w[1] for w in words], t)
        need = first // 2 ** 22
        lax.fori_loop(have, need, arrive, 0)
        for code in (first % 2048, (first // 2048) % 2048, second % 2048):
            who = decode(code)
            unit(who, before)
            before = who
        finish_all(before)
        ready = second // 2048
        lax.fori_loop(sent, ready, send_partial, 0)
        return (need, ready) + before

    prepare(0)
    zero = jnp.int32(0)
    carry = lax.fori_loop(0, len(words), trip, (zero + 1, zero, zero, zero, zero, zero + n_slots, zero + n_slots))
    for step in range(STEPS - LAG, STEPS):
        products(step, carry[2:])
    finish_all(carry[2:])
    lax.fori_loop(carry[1], n_slots - 1, send_partial, 0)

    out_ref[...] = yt[0]
    for slot in range(1, n_slots):
        y_copy(slot, me).wait_recv()
        out_ref[...] += yrecv[slot]
    for slot in range(1, n_slots):
        x_copy(slot, me).wait_send()
        v_copy(slot, me).wait_send()
        y_copy(slot, me).wait_send()


def solution(mesh):
    row_spec = P(('tasks', 'group'), None)
    offsets, finished, words = make_plan()
    n_slots = len(offsets)

    def local_fn(x_loc, v_loc, lengthscale, outscale):
        scale = -1.4426950408889634 / (2.0 * jnp.square(lengthscale))
        smem = pl.BlockSpec(memory_space=pltpu.SMEM)
        vmem = pl.BlockSpec(memory_space=pltpu.VMEM)
        dma = pltpu.SemaphoreType.DMA((n_slots,))
        y_t = pl.pallas_call(
            functools.partial(kernel, offsets, finished, words),
            out_shape=jax.ShapeDtypeStruct((RHS, ROWS), F32),
            in_specs=[smem, smem, vmem, vmem],
            out_specs=vmem,
            scratch_shapes=[
                pltpu.VMEM((n_slots, ROWS, FEAT), BF16),
                pltpu.VMEM((n_slots, ROWS // PANEL, RHS, PANEL), BF16),
                pltpu.VMEM((n_slots, 2, ROWS, FEAT), BF16),
                pltpu.VMEM((n_slots, ROWS // PANEL, 2 * FEAT, PANEL), BF16),
                pltpu.VMEM((n_slots + 1, RHS, ROWS), F32),
                pltpu.VMEM((n_slots, RHS, ROWS), F32),
                pltpu.VMEM((STEPS, 2, TILE, PANEL), BF16),
                pltpu.VMEM((STEPS, 2, TILE, PANEL), BF16),
                dma, dma, dma, dma, dma, dma,
            ],
            compiler_params=pltpu.CompilerParams(
                collective_id=0, has_side_effects=True, vmem_limit_bytes=60 * 1024 * 1024),
        )(scale, outscale, x_loc, v_loc.reshape(ROWS // PANEL, PANEL, RHS).transpose(0, 2, 1))
        return y_t.T

    return jax.shard_map(local_fn, mesh=mesh, in_specs=(row_spec, row_spec, P(None), P(None)),
                         out_specs=row_spec, check_vma=False)
```

time: 320 us -> 306 us (0.956)
  the two profiles are of different devices: /device:TPU:31 before, /device:TPU:15 now
where the time goes in v2:
time: 306 us
  Pallas kernels  302 us (99%)
    pallas_call x1, Pallas kernels, local_fn(): pl.pallas_call(functools.partial(kernel, offsets, finished, words), out_s...  302 us

profile of v2, /device:TPU:15, one launch (start us, length us, event | category | flops | bytes accessed | tf_op | source)
XLA Modules:
  0.0 305.6 jit_solution(9765902613111107433)
XLA Ops:
  0.0 0.0 copy-start
  1.4 0.0 copy-done
  1.4 0.7 bitcast_bitcast_fusion.v_ref
  2.1 301.7 %shard_map.46 = f32[64,1536]{1,0:T(8,128)} custom-call(f32[1]{0:T(128)S(6)} %div.3.c_ref, f32[1]{0:T(128)S(6)} %copy.10.s_ref, bf16[1536,128]{1,0:T(8,128)(2,1)} %x_ref.1, bf16[12,64,128]{2,1,0:T(8,128)(2,1)} %bitcast_bitcast_fusion.v_ref), custom_call_target="tpu_custom_call" | custom-call | tf_op jit(solution)/shard_map/pallas_call | solution.py:281
  303.8 1.8 copy.11
Async XLA Ops:
  0.0 1.4 copy-start

commit v3 on v2

--- a/solution.py
+++ b/solution.py
@@ -7,7 +7,15 @@
 from jax.experimental.pallas import tpu as pltpu
 from jax.sharding import PartitionSpec as P
 
-OFFSETS = (0, 6, 7, 21, 26, 31, 33, 37, 49, 53, 73, 88, 96, 97)
+OFFSETS = (0, 2, 6, 7, 18, 24, 25, 44, 65, 66, 82, 96, 113, 125)
+PAIRS = ((1, 0), (2, 1), (3, 1), (3, 0), (3, 2), (4, 3), (4, 0), (4, 1), (5, 0), (5, 1),
+         (6, 1), (6, 5), (7, 4), (7, 0), (8, 2), (8, 1), (8, 4), (9, 3), (9, 8), (9, 2),
+         (9, 4), (10, 6), (10, 0), (11, 4), (10, 7), (12, 6), (12, 2), (13, 3), (12, 5), (13, 4),
+         (12, 0), (10, 5), (11, 5), (12, 10), (10, 4), (13, 5), (9, 5), (9, 1), (8, 7), (12, 11),
+         (12, 8), (13, 2), (10, 1), (13, 7), (9, 0), (11, 9), (11, 7), (8, 3), (12, 1), (10, 2),
+         (12, 9), (11, 8), (7, 6), (6, 4), (7, 5), (13, 6), (12, 4), (8, 6), (11, 1), (7, 1),
+         (12, 7), (9, 6), (10, 8), (13, 0), (8, 0), (13, 10), (13, 11), (11, 10), (6, 0), (11, 6),
+         (11, 0))
 ROWS = 1536
 HALF = 768
 UNROLL = 3
@@ -38,39 +46,32 @@
 def make_plan():
     offsets = sorted(OFFSETS, key=lambda a: (hops(a), a))
     n_slots = len(offsets)
-    units = [(0, 0, 6, 1), (0, 0, 7, 0)]
+    units = [(0, 0, 6), (0, 0, 7)]
     seen = {0}
-    for n in range(1, n_slots):
-        first = True
-        for m in range(n):
-            g, back = difference(offsets[n], offsets[m]), difference(offsets[m], offsets[n])
-            if g in seen:
-                continue
-            seen.update((g, back))
-            if g == back:
-                kinds = (2 + [k for k in range(4) if coords(g)[k]][0],)
-            else:
-                kinds = (0, 1)
-            for kind in kinds:
-                units.append((n, m, kind, 1 if first else 0))
-                first = False
-        assert not first
+    for n, m in PAIRS:
+        g, back = difference(offsets[n], offsets[m]), difference(offsets[m], offsets[n])
+        assert g not in seen
+        seen.update((g, back))
+        if g == back:
+            units.append((n, m, 2 + [k for k in range(4) if coords(g)[k]][0]))
+        else:
+            units += [(n, m, 0), (n, m, 1)]
     assert len(seen) == 128
     while len(units) % UNROLL:
-        units.append((0, 0, 6, 0))
+        units.append((0, 0, 6))
     trips = [units[t:t + UNROLL] for t in range(0, len(units), UNROLL)]
     last = {}
     for t, trip in enumerate(trips):
-        for i, j, _, _ in trip:
+        for i, j, _ in trip:
             last[i] = t
             last[j] = t
     finished = sorted(range(1, n_slots), key=lambda slot: (last[slot], slot))
     words = []
     need = 1
     for t, trip in enumerate(trips):
-        need = max([need] + [max(i, j) + 1 for i, j, _, _ in trip])
+        need = max([need] + [max(i, j) + 1 for i, j, _ in trip])
         sent = sum(last[slot] < t for slot in finished)
-        codes = [i + 16 * j + 256 * kind for i, j, kind, _ in trip]
+        codes = [i + 16 * j + 256 * kind for i, j, kind in trip]
         words.append((codes[0] + 2048 * codes[1] + 2 ** 22 * need, codes[2] + 2048 * sent))
     return offsets, finished, words
 

time: 306 us -> 286 us (0.935)
  the two profiles are of different devices: /device:TPU:15 before, /device:TPU:13 now
where the time goes in v3:
time: 286 us
  Pallas kernels  282 us (99%)
    pallas_call x1, Pallas kernels, local_fn(): pl.pallas_call(functools.partial(kernel, offsets, finished, words), out_s...  282 us

profile of v3, /device:TPU:13, one launch (start us, length us, event | category | flops | bytes accessed | tf_op | source)
XLA Modules:
  0.0 286.1 jit_solution(14367103397501718164)
XLA Ops:
  0.0 0.0 copy-start
  1.4 0.0 copy-done
  1.4 0.7 bitcast_bitcast_fusion.v_ref
  2.1 282.2 %shard_map.46 = f32[64,1536]{1,0:T(8,128)} custom-call(f32[1]{0:T(128)S(6)} %div.3.c_ref, f32[1]{0:T(128)S(6)} %copy.10.s_ref, bf16[1536,128]{1,0:T(8,128)(2,1)} %x_ref.1, bf16[12,64,128]{2,1,0:T(8,128)(2,1)} %bitcast_bitcast_fusion.v_ref), custom_call_target="tpu_custom_call" | custom-call | tf_op jit(solution)/shard_map/pallas_call | solution.py:282
  284.3 1.8 copy.11
Async XLA Ops:
  0.0 1.4 copy-start

commit v4 on v3

--- a/solution.py
+++ b/solution.py
@@ -8,13 +8,13 @@
 from jax.sharding import PartitionSpec as P
 
 OFFSETS = (0, 2, 6, 7, 18, 24, 25, 44, 65, 66, 82, 96, 113, 125)
-PAIRS = ((1, 0), (2, 1), (3, 1), (3, 0), (3, 2), (4, 3), (4, 0), (4, 1), (5, 0), (5, 1),
-         (6, 1), (6, 5), (7, 4), (7, 0), (8, 2), (8, 1), (8, 4), (9, 3), (9, 8), (9, 2),
-         (9, 4), (10, 6), (10, 0), (11, 4), (10, 7), (12, 6), (12, 2), (13, 3), (12, 5), (13, 4),
-         (12, 0), (10, 5), (11, 5), (12, 10), (10, 4), (13, 5), (9, 5), (9, 1), (8, 7), (12, 11),
-         (12, 8), (13, 2), (10, 1), (13, 7), (9, 0), (11, 9), (11, 7), (8, 3), (12, 1), (10, 2),
-         (12, 9), (11, 8), (7, 6), (6, 4), (7, 5), (13, 6), (12, 4), (8, 6), (11, 1), (7, 1),
-         (12, 7), (9, 6), (10, 8), (13, 0), (8, 0), (13, 10), (13, 11), (11, 10), (6, 0), (11, 6),
+PAIRS = ((2, 1), (2, 0), (3, 2), (3, 1), (3, 0), (4, 3), (4, 1), (4, 0), (5, 1), (5, 3),
+         (6, 4), (6, 1), (7, 4), (7, 0), (7, 6), (8, 6), (8, 2), (8, 1), (8, 3), (9, 3),
+         (9, 2), (9, 4), (10, 6), (10, 7), (10, 4), (11, 4), (11, 2), (11, 10), (12, 11), (12, 4),
+         (13, 5), (12, 5), (12, 8), (13, 3), (13, 2), (13, 8), (13, 6), (13, 4), (11, 9), (12, 6),
+         (11, 3), (13, 7), (10, 2), (12, 7), (13, 12), (12, 0), (7, 5), (13, 0), (11, 1), (10, 5),
+         (10, 1), (8, 0), (7, 1), (12, 9), (12, 10), (11, 7), (7, 3), (9, 5), (8, 7), (11, 8),
+         (13, 10), (10, 8), (9, 8), (10, 0), (11, 6), (9, 6), (6, 0), (6, 5), (11, 5), (5, 0),
          (11, 0))
 ROWS = 1536
 HALF = 768
@@ -260,7 +260,7 @@
     lax.fori_loop(carry[1], n_slots - 1, send_partial, 0)
 
     out_ref[...] = yt[0]
-    for slot in range(1, n_slots):
+    for slot in finished:
         y_copy(slot, me).wait_recv()
         out_ref[...] += yrecv[slot]
     for slot in range(1, n_slots):

time: 286 us -> 268 us (0.937)
  the two profiles are of different devices: /device:TPU:13 before, /device:TPU:32 now
where the time goes in v4:
time: 268 us
  Pallas kernels  264 us (99%)
    pallas_call x1, Pallas kernels, local_fn(): pl.pallas_call(functools.partial(kernel, offsets, finished, words), out_s...  264 us

profile of v4, /device:TPU:32, one launch (start us, length us, event | category | flops | bytes accessed | tf_op | source)
XLA Modules:
  0.0 267.9 jit_solution(4978816147724562286)
XLA Ops:
  0.0 0.0 copy-start
  1.4 0.0 copy-done
  1.4 0.7 bitcast_bitcast_fusion.v_ref
  2.1 264.0 %shard_map.46 = f32[64,1536]{1,0:T(8,128)} custom-call(f32[1]{0:T(128)S(6)} %div.3.c_ref, f32[1]{0:T(128)S(6)} %copy.10.s_ref, bf16[1536,128]{1,0:T(8,128)(2,1)} %x_ref.1, bf16[12,64,128]{2,1,0:T(8,128)(2,1)} %bitcast_bitcast_fusion.v_ref), custom_call_target="tpu_custom_call" | custom-call | tf_op jit(solution)/shard_map/pallas_call | solution.py:282
  266.1 1.8 copy.11
Async XLA Ops:
  0.0 1.4 copy-start
